TPU v7x, 256 devices: a whole 4x4x8 slice. The times are simulated.
256 devices in a mesh: row: 8 (over x, z_lo), col: 8 (over z_hi, core), depth: 4 (over y).
Axes of the slice: x: 4, y: 4, z: 8 (z_hi: 4, z_lo: 2; z = z_hi * 2 + z_lo), core: 2. Of those that a mesh axis runs over, the one named last changes fastest.
Arguments:
- alignment_matrix: bfloat16 [128, 768, 256], P('depth', 'col'), may hold values from -6 to 6
- twin_linear_matrix: bfloat16 [256, 64], replicated, may hold values from -0.375 to 0.375
- final_matrix: bfloat16 [1024, 128], replicated, may hold values from -2 to 2
- final_offset: float32 [128], replicated, may hold values from -3 to 3
- adjoint_incoming: bfloat16 [768, 768, 128], P('row', ('col', 'depth')), may hold values from -6 to 6
Outputs:
- contact_delta: bfloat16 [768, 768, 128], P('row', ('col', 'depth'))
- alignment_adjoint: float32 [128, 768, 256], P('depth', 'col')
- grad_w_out: float32 [1024, 128], replicated
- grad_b_out: float32 [128], replicated
All inputs are finite; a program needn't handle non-finite values.
Results may differ from a plain program's by a relative error of at most 0.007.
Values may be sent and summed in bfloat16 or wider, within the bound.
No kernel may reach another device: no remote copies, remote signals or barrier semaphores. Data moves between devices by JAX's collectives and lax.ppermute only.
A program may use at most 128 MiB of HBM per device.

v0:
```python
import jax
import jax.numpy as jnp
from jax import lax
from jax.sharding import PartitionSpec as P

epsilon = 1e-05


def in_one(arrays, axis):
    vector, at, gathered = (jnp.concatenate([a.reshape(-1) for a in arrays]), 0, [])
    running = lax.psum(vector, axis)
    for a in arrays:
        gathered.append(running[at : at + a.size].reshape(a.shape))
        at += a.size
    return tuple(gathered)


def broadcast(shard, axis, root):
    return lax.dynamic_index_in_dim(lax.all_gather(shard, axis), root, 0, keepdims=False)


def copy_for_each(shard, axis):
    copies = jnp.broadcast_to(shard, (lax.axis_size(axis), *shard.shape))
    return lax.all_to_all(copies, axis, split_axis=0, concat_axis=0, tiled=True)


def of_everyone(shard, axis):
    everything = copy_for_each(shard, axis)
    return jnp.sum(everything, axis=0)


def standardize_channels(values):
    centre = jnp.mean(values, axis=-1, keepdims=True)
    spread = jnp.mean(jnp.square(values - centre), axis=-1, keepdims=True)
    return (values - centre) * lax.rsqrt(spread + epsilon)


def body(alignment_matrix, twin_linear_matrix, final_matrix, final_offset, adjoint_incoming):
    alignment_share, amino_share, discarded_item = alignment_matrix.shape
    latent_features = twin_linear_matrix.shape[1] // 2
    row_count = lax.axis_size("row")
    col_count = lax.axis_size("col")
    depth_count = lax.axis_size("depth")
    crop_length = amino_share * col_count
    block_i = crop_length // row_count
    quarter = amino_share // depth_count
    row_idx = lax.axis_index("row")
    col_idx = lax.axis_index("col")
    standardized_alignment, standardize_backprop = jax.vjp(
        standardize_channels, alignment_matrix.astype(jnp.float32)
    )
    normed = standardized_alignment.astype(jnp.bfloat16)
    panels = jnp.dot(normed, twin_linear_matrix, preferred_element_type=jnp.float32).astype(
        jnp.bfloat16
    )
    left_local = panels[..., :latent_features]
    right_local = panels[..., latent_features:]
    left_every = lax.all_gather(left_local, "col", axis=1, tiled=True)
    left_rows = lax.dynamic_slice_in_dim(left_every, row_idx * block_i, block_i, 1)
    left_seqs = lax.all_gather(left_rows, "depth", axis=0, tiled=True)
    right_seqs = lax.all_to_all(right_local, "depth", split_axis=1, concat_axis=0, tiled=True)
    seq_count = left_seqs.shape[0]
    summed = jnp.einsum(
        "sje,sic->jice", right_seqs, left_seqs, preferred_element_type=jnp.float32
    ).reshape(quarter, block_i, latent_features * latent_features)
    outer_mean = (summed / seq_count).astype(jnp.bfloat16)
    pair_cols = jnp.dot(outer_mean, final_matrix, preferred_element_type=jnp.float32) + final_offset
    contact_delta = jnp.transpose(pair_cols, (1, 0, 2)).astype(jnp.bfloat16)
    adjoint_kronecker = (
        jnp.einsum(
            "gtz,vz->gtv", adjoint_incoming, final_matrix, preferred_element_type=jnp.float32
        )
        / seq_count
    ).astype(jnp.bfloat16)
    grad_four = adjoint_kronecker.reshape(block_i, quarter, latent_features, latent_features)
    adjoint_leftside = jnp.einsum(
        "ijce,sje->sic", grad_four, right_seqs, preferred_element_type=jnp.float32
    )
    grad_right = jnp.einsum(
        "ijce,sic->sje", grad_four, left_seqs, preferred_element_type=jnp.float32
    )
    w_local = jnp.einsum(
        "jif,ijo->fo", outer_mean, adjoint_incoming, preferred_element_type=jnp.float32
    )
    b_local = jnp.sum(adjoint_incoming.astype(jnp.float32), axis=(0, 1))
    weight_gradient, bias_gradient = in_one((w_local, b_local), ("row", "col", "depth"))
    left_back, right_back = (
        lax.all_to_all(adjoint_leftside, "depth", split_axis=0, concat_axis=1, tiled=True),
        lax.all_to_all(grad_right, "depth", split_axis=0, concat_axis=1, tiled=True),
    )
    left_back = jnp.sum(
        left_back.reshape(alignment_share, depth_count, block_i, latent_features), axis=1
    )
    left_summed = lax.psum(left_back, "col")
    owner_row = col_idx * amino_share // block_i
    left_full = broadcast(left_summed.astype(jnp.bfloat16), "row", owner_row).astype(
        left_summed.dtype
    )
    right_full = of_everyone(right_back, "row")
    both_grads = jnp.concatenate([left_full, right_full], axis=-1)
    grad_panels = both_grads.astype(jnp.bfloat16)
    standardized_adjoint = jnp.einsum(
        "slk,mk->slm", grad_panels, twin_linear_matrix, preferred_element_type=jnp.float32
    )
    alignment_adjoint = standardize_backprop(standardized_adjoint)[0]
    return (
        contact_delta,
        alignment_adjoint,
        weight_gradient / crop_length,
        bias_gradient / crop_length,
    )


def solution(mesh):
    in_specs = (P("depth", "col", None), P(), P(), P(), P("row", ("col", "depth"), None))
    out_specs = (P("row", ("col", "depth"), None), P("depth", "col", None), P(), P())
    return jax.shard_map(body, mesh=mesh, in_specs=in_specs, out_specs=out_specs, check_vma=False)
```

profile of v0, /device:TPU:1, one launch (start us, length us, event | category | flops | bytes accessed | tf_op | source)
XLA Modules:
  0.0 472.1 jit_solution(5661845479301086679)
XLA Ops:
  8.1 2.1 convert_reduce_fusion
  10.2 2.4 fusion.8
  12.7 1.3 fusion.16
  14.1 2.0 copy.31
  16.2 1.2 copy.33
  17.4 1.4 reshape.73
  18.8 5.0 %all-to-all-start = ((bf16[4,2,12288]{2,1,0:T(2,128)(2,1)}), bf16[4,2,12288]{2,1,0:T(2,128)(2,1)S(1)}, u32[]{:S(2)}, u32[]{:S(2)}) async-start(bf16[4,2,12288]{2,1,0:T(2,128)(2,1)} %reshape.73), calls=%async_computation | async-start | bytes 393216 | tf_op jit(solution)/shard_map/all_to_all | solution.py:61
  23.8 3.5 multiply_convert_fusion.1
  27.3 8.5 %copy.39 = bf16[96,24,1024]{0,2,1:T(8,128)(2,1)} copy(bf16[96,24,1024]{2,1,0:T(8,128)(2,1)} %multiply_convert_fusion.1) | data formatting | bytes 9437184 | tf_op jit(solution)/shard_map/convert_element_type | solution.py:74
  35.8 0.4 reshape.74
  36.2 0.6 copy.56
  36.8 1.1 reshape.66
  37.9 5.1 %convolution_bitcast_fusion.1 = f32[128,96,32]{0,1,2:T(8,128)S(1)} fusion(bf16[96,24,32,32]{0,3,2,1:T(8,128)(2,1)} %bitcast.63, bf16[128,24,32,1]{0,2,1,3:T(8,128)(2,1)} %reshape.66), kind=kOutput, calls=%fused_computation.20 | convolution fusion | flops 603979776 | bytes 6488064 | tf_op jit(solution)/shard_map/ijce,sje->sic/dot_general | solution.py:76
  43.0 1.9 copy.41
  44.9 4.8 %all-to-all-start.1 = ((f32[128,96,32]{1,2,0:T(8,128)}), f32[128,96,32]{1,2,0:T(8,128)}, u32[]{:S(2)}, u32[]{:S(2)}) async-start(f32[128,96,32]{1,2,0:T(8,128)} %copy.41), calls=%async_computation.1 | async-start | bytes 4194304 | tf_op jit(solution)/shard_map/all_to_all | solution.py:88
  50.0 24.5 %all-to-all-done.1 = f32[128,96,32]{1,2,0:T(8,128)} async-done(((f32[128,96,32]{1,2,0:T(8,128)}), f32[128,96,32]{1,2,0:T(8,128)}, u32[]{:S(2)}, u32[]{:S(2)}) %all-to-all-start.1) | async-done | bytes 1572896 | tf_op jit(solution)/shard_map/all_to_all | solution.py:88
  74.6 2.7 reduce_sum.82
  77.3 13.4 %all-gather.4.cloned.1.call-done = bf16[32,768,32]{2,0,1:T(8,128)(2,1)} async-done(((bf16[32,96,32]{2,0,1:T(8,128)(2,1)}), bf16[32,768,32]{2,0,1:T(8,128)(2,1)}) %all-gather.4.cloned.1.call-update) | async-done | bytes 1572880 | tf_op jit(solution)/shard_map/all_gather | solution.py:58
  90.6 1.2 constant_dynamic-slice_fusion
  91.8 0.8 copy.32
  92.6 13.8 %all_gather.13 = bf16[128,96,32]{1,2,0:T(8,128)(2,1)S(1)} all-gather(bf16[32,96,32]{1,2,0:T(8,128)(2,1)S(1)} %copy.32), channel_id=1, replica_groups=mesh['row'=8,'col'=8,'depth'=4] {'depth'}, dimensions={0}, use_global_device_ids=true | all-gather | bytes 983040 | tf_op jit(solution)/shard_map/all_gather | solution.py:60
  106.4 5.0 %convolution_bitcast_fusion.2 = f32[128,24,32]{0,2,1:T(8,128)S(1)} fusion(bf16[96,24,32,32]{0,3,2,1:T(8,128)(2,1)} %bitcast.64, bf16[128,96,32]{1,2,0:T(8,128)(2,1)S(1)} %all_gather.13), kind=kOutput, calls=%fused_computation.25 | convolution fusion | flops 603979776 | bytes 5898240 | tf_op jit(solution)/shard_map/ijce,sic->sje/dot_general | solution.py:79
  111.4 2.4 copy.48
  113.9 1.6 copy.43
  115.5 2.8 reshape.75
  118.3 3.5 all-to-all-start.2
  121.8 9.1 %fusion = bf16[24,96,32,32]{3,2,0,1:T(8,128)(2,1)} fusion(bf16[128,96,32,1]{0,2,3,1:T(8,128)(2,1)S(1)} %copy.48, bf16[128,24,32,1]{0,2,1,3:T(8,128)(2,1)S(1)} %copy-done.7), kind=kOutput, calls=%fused_computation.1 | convolution fusion | flops 608698368 | bytes 5701632 | tf_op jit(solution)/shard_map/sje,sic->jice/dot_general | solution.py:63
  130.9 20.1 %copy.37 = bf16[24,96,32,32]{1,3,2,0:T(8,128)(2,1)} copy(bf16[24,96,32,32]{3,2,0,1:T(8,128)(2,1)} %fusion) | data formatting | bytes 9437184 | tf_op jit(solution)/shard_map/convert_element_type | solution.py:66
  151.0 0.5 broadcast.58
  151.5 2.5 reduce.2
  154.0 1.5 reshape.76
  155.5 1.8 copy.44
  157.4 2.4 all_to_all.47
  159.8 2.5 broadcast_in_dim.4
  162.3 4.7 all-to-all-start.3
  167.3 4.3 convolution_bitcast_fusion
  171.6 0.8 pad_maximum_fusion
  172.6 66.0 %all-reduce.4 = bf16[32,96,32]{1,2,0:T(8,128)(2,1)} all-reduce(f32[32,96,32]{1,2,0:T(8,128)S(1)} %copy-done.6), channel_id=1, replica_groups=mesh['row'=8,'col'=8,'depth'=4] {'col'}, use_global_device_ids=true, to_apply=%region_3.0 | all-reduce | flops 98304 | bytes 589824 | tf_op jit(solution)/shard_map/psum | solution.py:94
  238.7 4.6 fusion.19
  243.3 1.0 copy.47
  244.3 205.4 %all-reduce.3.cloned.1.call-done = f32[131200]{0:T(1024)} async-done(((f32[131200]{0:T(1024)}), f32[131200]{0:T(1024)}) %all-reduce.3.cloned.1.call-update) | async-done | bytes 524816 | tf_op jit(solution)/shard_map/psum | solution.py:11
  449.8 1.2 slice_multiply_fusion.1
  450.9 1.9 fusion.23
  452.8 1.0 dynamic-slice_bitcast_fusion
  453.8 2.8 reduce_sum.83
  456.6 3.2 multiply_reduce_fusion
  459.9 1.6 fusion.5
  461.5 3.2 fusion.7
  (36 shorter events, 0.9 us)
Async XLA Ops:
  8.0 15.8 %copy-start = (bf16[1024,128]{1,0:T(8,128)(2,1)S(1)}, bf16[1024,128]{1,0:T(8,128)(2,1)}, u32[]{:S(2)}) copy-start(bf16[1024,128]{1,0:T(8,128)(2,1)} %param.7) | copy-start | bytes 786436
  8.0 4.7 copy-start.1
  8.0 4.7 copy-start.8
  8.0 82.6 %all-gather.4.cloned.1.call-start = ((), (), s32[]{:S(2)}) async-start(), calls=%async_computation.4 | async-start | bytes 7077888 | tf_op jit(solution)/shard_map/all_gather | solution.py:58
  14.1 9.8 %copy-start.3 = (bf16[96,24,128]{2,1,0:T(8,128)(2,1)S(1)}, bf16[96,24,128]{2,1,0:T(8,128)(2,1)}, u32[]{:S(2)}) copy-start(bf16[96,24,128]{2,1,0:T(8,128)(2,1)} %param.9) | copy-start | bytes 1769476
  18.8 17.0 %all-to-all-start = ((bf16[4,2,12288]{2,1,0:T(2,128)(2,1)}), bf16[4,2,12288]{2,1,0:T(2,128)(2,1)S(1)}, u32[]{:S(2)}, u32[]{:S(2)}) async-start(bf16[4,2,12288]{2,1,0:T(2,128)(2,1)} %reshape.73), calls=%async_computation | async-start | bytes 393216 | tf_op jit(solution)/shard_map/all_to_all | solution.py:61
  44.9 4.8 %copy-start.4 = (bf16[96,24,128]{2,1,0:T(8,128)(2,1)S(1)}, bf16[96,24,128]{2,1,0:T(8,128)(2,1)}, u32[]{:S(2)}) copy-start(bf16[96,24,128]{2,1,0:T(8,128)(2,1)} %param.9) | copy-start | bytes 1769476
  44.9 29.7 %all-to-all-start.1 = ((f32[128,96,32]{1,2,0:T(8,128)}), f32[128,96,32]{1,2,0:T(8,128)}, u32[]{:S(2)}, u32[]{:S(2)}) async-start(f32[128,96,32]{1,2,0:T(8,128)} %copy.41), calls=%async_computation.1 | async-start | bytes 4194304 | tf_op jit(solution)/shard_map/all_to_all | solution.py:88
  106.4 5.0 %copy-start.2 = (bf16[128,96,32]{1,2,0:T(8,128)(2,1)}, bf16[128,96,32]{1,2,0:T(8,128)(2,1)S(1)}, u32[]{:S(2)}) copy-start(bf16[128,96,32]{1,2,0:T(8,128)(2,1)S(1)} %all_gather.13) | copy-start | bytes 2359300
  111.4 10.4 %copy-start.7 = (bf16[128,24,32,1]{0,2,1,3:T(8,128)(2,1)S(1)}, bf16[128,24,32,1]{0,2,1,3:T(8,128)(2,1)}, u32[]{:S(2)}) copy-start(bf16[128,24,32,1]{0,2,1,3:T(8,128)(2,1)} %reshape.66) | copy-start | bytes 589828
  118.3 32.7 %all-to-all-start.2 = ((f32[4,1,24576]{2,1,0:T(1,128)}), f32[4,1,24576]{2,1,0:T(1,128)S(1)}, u32[]{:S(2)}, u32[]{:S(2)}) async-start(f32[4,1,24576]{2,1,0:T(1,128)} %reshape.75), calls=%async_computation.2 | async-start | bytes 786432 | tf_op jit(solution)/shard_map/all_to_all | solution.py:89
  162.3 5.0 %copy-start.5 = (bf16[96,24,128]{2,1,0:T(8,128)(2,1)S(1)}, bf16[96,24,128]{2,1,0:T(8,128)(2,1)}, u32[]{:S(2)}) copy-start(bf16[96,24,128]{2,1,0:T(8,128)(2,1)} %param.9) | copy-start | bytes 1769476
  162.3 291.5 %all-to-all-start.3 = ((f32[8,32,96,32]{2,3,1,0:T(8,128)}), f32[8,32,96,32]{2,3,1,0:T(8,128)}, u32[]{:S(2)}, u32[]{:S(2)}) async-start(f32[8,32,96,32]{2,3,1,0:T(8,128)} %broadcast_in_dim.4), calls=%async_computation.3 | async-start | bytes 8388608 | tf_op jit(solution)/shard_map/all_to_all | solution.py:24
  167.0 282.8 %all-reduce.3.cloned.1.call-start = ((), (), s32[]{:S(2)}) async-start(), calls=%async_computation.5 | async-start | bytes 1056768 | tf_op jit(solution)/shard_map/psum | solution.py:11
  167.3 5.3 %copy-start.6 = (f32[32,96,32]{1,2,0:T(8,128)S(1)}, f32[32,96,32]{1,2,0:T(8,128)}, u32[]{:S(2)}) copy-start(f32[32,96,32]{1,2,0:T(8,128)} %reduce_sum.82) | copy-start | bytes 1179652
  167.3 71.4 %copy-start.9 = (f32[128]{0:T(128)S(1)}, f32[128]{0:T(128)}, u32[]{:S(2)}) copy-start(f32[128]{0:T(128)} %param.8) | copy-start | bytes 1540
  172.5 280.3 %all-gather.6.cloned.1.call-start = ((), (), s32[]{:S(2)}) async-start(), calls=%async_computation.6 | async-start | bytes 2359296 | tf_op jit(solution)/shard_map/all_gather | solution.py:19
Sparse Core Ops, SparseCore 0:
  16.3 74.2 all-gather.3
  173.9 275.8 all-reduce.2
Sparse Core Ops, SparseCore 1:
  238.7 60.2 all-gather.5
where the time goes:
time: 474 us; the launch traced here: 472 us
  waiting for transfers between devices  243 us (51%)
  blocking collectives  79.8 us (17%)
  local copies, waits for them, and re-layouts  57 us (12%)
  matrix products  36.2 us (8%)
  other arithmetic  21.6 us (5%)
  starting transfers between devices  18.3 us (4%)
  between operations  15.8 us (3%)
    psum x1, waiting for transfers between devices, in_one(): running = lax.psum(vector, axis)  205 us
    psum x1, blocking collectives, body(): left_summed = lax.psum(left_back, 'col')  66 us
    all_to_all x1, waiting for transfers between devices, body(): lax.all_to_all(adjoint_leftside, 'depth', split_axis=0, concat_axis=1, ti...  24.5 us
    convert_element_type x1, local copies, waits for them, and re-layouts, body(): outer_mean = (summed / seq_count).astype(jnp.bfloat16)  20.1 us
    all_gather x1, blocking collectives, body(): left_seqs = lax.all_gather(left_rows, 'depth', axis=0, tiled=True)  13.8 us
    all_gather x1, waiting for transfers between devices, body(): left_every = lax.all_gather(left_local, 'col', axis=1, tiled=True)  13.4 us
  transfers between devices with their start and end apart: 7, of which 3 were waited for; matrix products, arithmetic and copies ran while one was open for 15% of the time, Pallas kernels for 0%

commit v1 on v0

--- a/solution.py
+++ b/solution.py
@@ -36,6 +36,18 @@
 
 
 def body(alignment_matrix, twin_linear_matrix, final_matrix, final_offset, adjoint_incoming):
+
+    def name_screen_for(frame_in, d_out, array_axis, link_axis):
+        return jnp.concatenate(
+            lax.all_to_all(
+                jnp.stack(jnp.split(frame_in, lax.psum(1, axis_name=link_axis), axis=array_axis)),
+                axis_name=link_axis,
+                split_axis=0,
+                concat_axis=0,
+            ),
+            axis=d_out,
+        )
+
     alignment_share, amino_share, discarded_item = alignment_matrix.shape
     latent_features = twin_linear_matrix.shape[1] // 2
     row_count = lax.axis_size("row")
@@ -85,7 +97,7 @@
     b_local = jnp.sum(adjoint_incoming.astype(jnp.float32), axis=(0, 1))
     weight_gradient, bias_gradient = in_one((w_local, b_local), ("row", "col", "depth"))
     left_back, right_back = (
-        lax.all_to_all(adjoint_leftside, "depth", split_axis=0, concat_axis=1, tiled=True),
+        name_screen_for(adjoint_leftside, 1, 0, "depth"),
         lax.all_to_all(grad_right, "depth", split_axis=0, concat_axis=1, tiled=True),
     )
     left_back = jnp.sum(

time: 474 us -> 481 us (1.015)
  waiting for transfers between devices: 243 us -> 231 us
  local copies, waits for them, and re-layouts: 57 us -> 68.2 us
    all_gather x1, waiting for transfers between devices: 13.4 us -> 0.01 us  [body(): left_every = lax.all_gather(left_local, 'col', axis=1, tiled=True)]
    another operation x0 -> x5, local copies, waits for them, and re-layouts: none -> 13.1 us  [name_screen_for(): jnp.stack(jnp.split(frame_in, lax.psum(1, axis_name=link_axis), axis=arra...]
  transfers between devices with their start and end apart: 7 -> 7, of which waited for: 3 -> 2; matrix products, arithmetic and copies ran while one was open for 15% -> 18% of each run, Pallas kernels for 0% -> 0%
where the time goes in v1:
time: 481 us; the launch traced here: 479 us
  waiting for transfers between devices  231 us (48%)
  blocking collectives  83.5 us (17%)
  local copies, waits for them, and re-layouts  68.2 us (14%)
  matrix products  36.1 us (8%)
  other arithmetic  24.7 us (5%)
  starting transfers between devices  19.1 us (4%)
  between operations  15.9 us (3%)
    psum x1, waiting for transfers between devices, in_one(): running = lax.psum(vector, axis)  207 us
    psum x1, blocking collectives, body(): left_summed = lax.psum(left_back, 'col')  70.2 us
    all_to_all x1, waiting for transfers between devices, name_screen_for(): lax.all_to_all(jnp.stack(jnp.split(frame_in, lax.psum(1, axis_name=link_a...  24.4 us
    convert_element_type x1, local copies, waits for them, and re-layouts, body(): outer_mean = (summed / seq_count).astype(jnp.bfloat16)  20.1 us
    all_gather x1, blocking collectives, body(): left_seqs = lax.all_gather(left_rows, 'depth', axis=0, tiled=True)  13.2 us
    another operation x5, local copies, waits for them, and re-layouts, name_screen_for(): jnp.stack(jnp.split(frame_in, lax.psum(1, axis_name=link_axis), axis=arra...  13.1 us
  transfers between devices with their start and end apart: 7, of which 2 were waited for; matrix products, arithmetic and copies ran while one was open for 18% of the time, Pallas kernels for 0%

profile of v1, /device:TPU:1, one launch (start us, length us, event | category | flops | bytes accessed | tf_op | source)
XLA Modules:
  0.0 478.8 jit_solution(18174001018659778824)
XLA Ops:
  8.1 2.1 convert_reduce_fusion
  10.2 2.4 fusion.8
  12.7 1.3 fusion.16
  14.1 2.0 copy.52
  16.2 1.2 copy.54
  17.4 1.4 reshape.72
  18.8 5.0 %all-to-all-start = ((bf16[4,2,12288]{2,1,0:T(2,128)(2,1)}), bf16[4,2,12288]{2,1,0:T(2,128)(2,1)S(1)}, u32[]{:S(2)}, u32[]{:S(2)}) async-start(bf16[4,2,12288]{2,1,0:T(2,128)(2,1)} %reshape.72), calls=%async_computation | async-start | bytes 393216 | tf_op jit(solution)/shard_map/all_to_all | solution.py:73
  23.8 3.5 multiply_convert_fusion.1
  27.4 8.5 %copy.60 = bf16[96,24,1024]{0,2,1:T(8,128)(2,1)} copy(bf16[96,24,1024]{2,1,0:T(8,128)(2,1)} %multiply_convert_fusion.1) | data formatting | bytes 9437184 | tf_op jit(solution)/shard_map/convert_element_type | solution.py:86
  37.9 5.0 %convolution_bitcast_fusion.1 = f32[128,96,32]{0,1,2:T(8,128)S(1)} fusion(bf16[96,24,32,32]{0,3,2,1:T(8,128)(2,1)} %bitcast.70, bf16[128,24,32,1]{0,2,1,3:T(8,128)(2,1)S(1)} %reshape.65), kind=kOutput, calls=%fused_computation.25 | convolution fusion | flops 603979776 | bytes 6488064 | tf_op jit(solution)/shard_map/ijce,sje->sic/dot_general | solution.py:88
  42.9 3.5 slice_bitcast_fusion.3
  46.5 2.7 copy.65
  49.2 2.7 copy.64
  51.9 2.7 copy.63
  54.6 1.3 copy.62
  56.0 3.1 pad_maximum_fusion
  59.1 4.6 all-to-all-start.1
  64.0 24.4 %all-to-all-done.1 = f32[4,32,96,32]{2,3,1,0:T(8,128)} async-done(((f32[4,32,96,32]{2,3,1,0:T(8,128)}), f32[4,32,96,32]{2,3,1,0:T(8,128)}, u32[]{:S(2)}, u32[]{:S(2)}) %all-to-all-start.1) | async-done | bytes 1572896 | tf_op jit(solution)/shard_map/all_to_all | solution.py:42
  88.4 2.7 reduce_sum.82
  91.1 1.2 constant_dynamic-slice_fusion
  92.3 0.8 copy.53
  93.1 13.2 %all_gather.13 = bf16[128,96,32]{1,2,0:T(8,128)(2,1)S(1)} all-gather(bf16[32,96,32]{1,2,0:T(8,128)(2,1)S(1)} %copy.53), channel_id=1, replica_groups=mesh['row'=8,'col'=8,'depth'=4] {'depth'}, dimensions={0}, use_global_device_ids=true | all-gather | bytes 983040 | tf_op jit(solution)/shard_map/all_gather | solution.py:72
  106.4 5.0 %convolution_bitcast_fusion.2 = f32[128,24,32]{0,2,1:T(8,128)S(1)} fusion(bf16[96,24,32,32]{0,3,2,1:T(8,128)(2,1)} %bitcast.71, bf16[128,96,32]{1,2,0:T(8,128)(2,1)S(1)} %all_gather.13), kind=kOutput, calls=%fused_computation.30 | convolution fusion | flops 603979776 | bytes 5898240 | tf_op jit(solution)/shard_map/ijce,sic->sje/dot_general | solution.py:91
  111.3 2.4 copy.74
  113.8 1.6 copy.69
  115.4 2.8 reshape.74
  118.2 3.5 all-to-all-start.2
  121.7 9.1 %fusion = bf16[24,96,32,32]{3,2,0,1:T(8,128)(2,1)} fusion(bf16[128,96,32,1]{0,2,3,1:T(8,128)(2,1)S(1)} %copy.74, bf16[128,24,32,1]{0,2,1,3:T(8,128)(2,1)S(1)} %copy-done.8), kind=kOutput, calls=%fused_computation.1 | convolution fusion | flops 608698368 | bytes 5701632 | tf_op jit(solution)/shard_map/sje,sic->jice/dot_general | solution.py:75
  130.8 20.1 %copy.58 = bf16[24,96,32,32]{1,3,2,0:T(8,128)(2,1)} copy(bf16[24,96,32,32]{3,2,0,1:T(8,128)(2,1)} %fusion) | data formatting | bytes 9437184 | tf_op jit(solution)/shard_map/convert_element_type | solution.py:78
  151.4 2.5 reduce.1
  153.9 1.5 reshape.75
  155.4 1.8 copy.70
  157.3 2.4 all_to_all.40
  159.7 2.5 broadcast_in_dim.4
  162.2 5.9 %all-to-all-start.3 = ((f32[8,32,96,32]{2,3,1,0:T(8,128)}), f32[8,32,96,32]{2,3,1,0:T(8,128)}, u32[]{:S(2)}, u32[]{:S(2)}) async-start(f32[8,32,96,32]{2,3,1,0:T(8,128)} %broadcast_in_dim.4), calls=%async_computation.3 | async-start | bytes 8388608 | tf_op jit(solution)/shard_map/all_to_all | solution.py:24
  168.2 4.3 convolution_bitcast_fusion
  172.5 0.8 pad_maximum_fusion.1
  173.5 70.2 %all-reduce.4 = bf16[32,96,32]{1,2,0:T(8,128)(2,1)} all-reduce(f32[32,96,32]{1,2,0:T(8,128)S(1)} %copy-done.6), channel_id=1, replica_groups=mesh['row'=8,'col'=8,'depth'=4] {'col'}, use_global_device_ids=true, to_apply=%region_3.0 | all-reduce | flops 98304 | bytes 589824 | tf_op jit(solution)/shard_map/psum | solution.py:106
  243.7 4.6 fusion.19
  248.4 1.0 copy.73
  249.4 207.0 %all-reduce.3.cloned.1.call-done = f32[131200]{0:T(1024)} async-done(((f32[131200]{0:T(1024)}), f32[131200]{0:T(1024)}) %all-reduce.3.cloned.1.call-update) | async-done | bytes 524816 | tf_op jit(solution)/shard_map/psum | solution.py:11
  456.5 1.2 slice_multiply_fusion.1
  457.6 1.9 fusion.23
  459.5 1.0 dynamic-slice_bitcast_fusion
  460.5 2.8 reduce_sum.83
  463.3 3.2 multiply_reduce_fusion
  466.6 1.6 fusion.5
  468.2 3.2 fusion.7
  (43 shorter events, 3.1 us)
Async XLA Ops:
  8.0 15.8 %copy-start = (bf16[1024,128]{1,0:T(8,128)(2,1)S(1)}, bf16[1024,128]{1,0:T(8,128)(2,1)}, u32[]{:S(2)}) copy-start(bf16[1024,128]{1,0:T(8,128)(2,1)} %param.7) | copy-start | bytes 786436
  8.0 4.7 copy-start.1
  8.0 4.7 copy-start.9
  8.0 83.1 %all-gather.4.cloned.1.call-start = ((), (), s32[]{:S(2)}) async-start(), calls=%async_computation.4 | async-start | bytes 7077888 | tf_op jit(solution)/shard_map/all_gather | solution.py:70
  14.1 9.8 %copy-start.3 = (bf16[96,24,128]{2,1,0:T(8,128)(2,1)S(1)}, bf16[96,24,128]{2,1,0:T(8,128)(2,1)}, u32[]{:S(2)}) copy-start(bf16[96,24,128]{2,1,0:T(8,128)(2,1)} %param.9) | copy-start | bytes 1769476
  18.8 17.0 %all-to-all-start = ((bf16[4,2,12288]{2,1,0:T(2,128)(2,1)}), bf16[4,2,12288]{2,1,0:T(2,128)(2,1)S(1)}, u32[]{:S(2)}, u32[]{:S(2)}) async-start(bf16[4,2,12288]{2,1,0:T(2,128)(2,1)} %reshape.72), calls=%async_computation | async-start | bytes 393216 | tf_op jit(solution)/shard_map/all_to_all | solution.py:73
  37.2 0.7 copy-start.7
  59.1 4.6 copy-start.4
  59.1 29.3 %all-to-all-start.1 = ((f32[4,32,96,32]{2,3,1,0:T(8,128)}), f32[4,32,96,32]{2,3,1,0:T(8,128)}, u32[]{:S(2)}, u32[]{:S(2)}) async-start(f32[4,32,96,32]{2,3,1,0:T(8,128)} %pad_maximum_fusion), calls=%async_computation.1 | async-start | bytes 4194304 | tf_op jit(solution)/shard_map/all_to_all | solution.py:42
  106.4 5.0 %copy-start.2 = (bf16[128,96,32]{1,2,0:T(8,128)(2,1)}, bf16[128,96,32]{1,2,0:T(8,128)(2,1)S(1)}, u32[]{:S(2)}) copy-start(bf16[128,96,32]{1,2,0:T(8,128)(2,1)S(1)} %all_gather.13) | copy-start | bytes 2359300
  111.3 10.4 %copy-start.8 = (bf16[128,24,32,1]{0,2,1,3:T(8,128)(2,1)S(1)}, bf16[128,24,32,1]{0,2,1,3:T(8,128)(2,1)}, u32[]{:S(2)}) copy-start(bf16[128,24,32,1]{0,2,1,3:T(8,128)(2,1)} %copy-done.7) | copy-start | bytes 589828
  118.2 32.7 %all-to-all-start.2 = ((f32[4,1,24576]{2,1,0:T(1,128)}), f32[4,1,24576]{2,1,0:T(1,128)S(1)}, u32[]{:S(2)}, u32[]{:S(2)}) async-start(f32[4,1,24576]{2,1,0:T(1,128)} %reshape.74), calls=%async_computation.2 | async-start | bytes 786432 | tf_op jit(solution)/shard_map/all_to_all | solution.py:101
  162.2 5.9 %copy-start.5 = (bf16[96,24,128]{2,1,0:T(8,128)(2,1)S(1)}, bf16[96,24,128]{2,1,0:T(8,128)(2,1)}, u32[]{:S(2)}) copy-start(bf16[96,24,128]{2,1,0:T(8,128)(2,1)} %param.9) | copy-start | bytes 1769476
  162.2 298.3 %all-to-all-start.3 = ((f32[8,32,96,32]{2,3,1,0:T(8,128)}), f32[8,32,96,32]{2,3,1,0:T(8,128)}, u32[]{:S(2)}, u32[]{:S(2)}) async-start(f32[8,32,96,32]{2,3,1,0:T(8,128)} %broadcast_in_dim.4), calls=%async_computation.3 | async-start | bytes 8388608 | tf_op jit(solution)/shard_map/all_to_all | solution.py:24
  168.1 288.3 %all-reduce.3.cloned.1.call-start = ((), (), s32[]{:S(2)}) async-start(), calls=%async_computation.5 | async-start | bytes 1056768 | tf_op jit(solution)/shard_map/psum | solution.py:11
  168.2 5.3 %copy-start.6 = (f32[32,96,32]{1,2,0:T(8,128)S(1)}, f32[32,96,32]{1,2,0:T(8,128)}, u32[]{:S(2)}) copy-start(f32[32,96,32]{1,2,0:T(8,128)} %reduce_sum.82) | copy-start | bytes 1179652
  168.2 75.6 %copy-start.10 = (f32[128]{0:T(128)S(1)}, f32[128]{0:T(128)}, u32[]{:S(2)}) copy-start(f32[128]{0:T(128)} %param.8) | copy-start | bytes 1540
  173.4 286.1 %all-gather.6.cloned.1.call-start = ((), (), s32[]{:S(2)}) async-start(), calls=%async_computation.6 | async-start | bytes 2359296 | tf_op jit(solution)/shard_map/all_gather | solution.py:19
Sparse Core Ops, SparseCore 0:
  16.3 74.3 all-gather.3
  175.0 281.3 all-reduce.2
Sparse Core Ops, SparseCore 1:
  243.8 61.8 all-gather.5
